TPU v7x, 128 devices: a whole 4x4x4 slice. The times are simulated.
128 devices in a mesh: data: 1, tp: 64 (over z, y, x), ep: 2 (over core).
Axes of the slice: x: 4, y: 4, z: 4, core: 2. Of those that a mesh axis runs over, the one named last changes fastest.
Arguments:
- tokens_a: bfloat16 [4096, 2048], P(('data', 'ep', 'tp'))
- tokens_b: bfloat16 [4096, 2048], P(('data', 'ep', 'tp'))
- experts_a: int32 [4096, 4], P(('data', 'ep', 'tp'))
- experts_b: int32 [4096, 4], P(('data', 'ep', 'tp'))
- gates_a: float32 [4096, 4], P(('data', 'ep', 'tp'))
- gates_b: float32 [4096, 4], P(('data', 'ep', 'tp'))
- slots_a: int32 [4096, 4], P(('data', 'ep', 'tp'))
- slots_b: int32 [4096, 4], P(('data', 'ep', 'tp'))
- shared_w1: bfloat16 [2048, 5632], P(None, 'tp')
- shared_w3: bfloat16 [2048, 5632], P(None, 'tp')
- shared_w2: bfloat16 [5632, 2048], P('tp')
- routed_w1: bfloat16 [60, 2048, 1408], P('ep')
- routed_w3: bfloat16 [60, 2048, 1408], P('ep')
- routed_w2: bfloat16 [60, 1408, 2048], P('ep')
Outputs:
- output 1: bfloat16 [4096, 2048], P(('data', 'ep', 'tp'))
- output 2: bfloat16 [4096, 2048], P(('data', 'ep', 'tp'))
All inputs are finite; a program needn't handle non-finite values.
Results may differ from a plain program's by a relative error of at most 0.0049404.
Values are sent between devices in bfloat16 or wider.
A program may use at most 1.5 GiB of HBM per device.

v0:
```python
import jax
import jax.numpy as jnp
from jax import lax
from jax.sharding import PartitionSpec as P


def capacity_rows(tok_local, top_k, num_experts):
    return max(4, (2 * tok_local * top_k) // num_experts)


def swiglu_rows(rows, w_in, w_gate, w_out):
    proj_in = jnp.dot(rows, w_in, preferred_element_type=jnp.float32)
    proj_gate = jnp.dot(rows, w_gate, preferred_element_type=jnp.float32)
    hidden = (jax.nn.silu(proj_in) * proj_gate).astype(jnp.bfloat16)
    return jnp.dot(hidden, w_out, preferred_element_type=jnp.float32)


def solution(mesh):
    ep_size = mesh.shape['ep']
    tok_spec = P(('data', 'ep', 'tp'), None)
    in_specs = (tok_spec,) * 8 + (P(None, 'tp'), P(None, 'tp'), P('tp', None), P('ep', None, None), P('ep', None, None), P('ep', None, None))

    def shared_path(x_local, shared_w1, shared_w3, shared_w2):
        gathered = lax.all_gather(x_local, 'tp', axis=0, tiled=True)
        partial_sum = swiglu_rows(gathered, shared_w1, shared_w3, shared_w2)
        return lax.psum_scatter(partial_sum, 'tp', scatter_dimension=0, tiled=True)

    def routed_path(x_local, expert_ids, gate_vals, slot_ids, routed_w1, routed_w3, routed_w2):
        tok_local, top_k = expert_ids.shape
        local_experts, model_dim, expert_ff = routed_w1.shape
        cap_rows = capacity_rows(tok_local, top_k, local_experts * ep_size)
        num_rows = local_experts * ep_size * cap_rows
        dest_rank = expert_ids // local_experts
        local_id = expert_ids % local_experts
        keep_mask = slot_ids >= 0
        row_ids = jnp.where(keep_mask, (local_id * ep_size + dest_rank) * cap_rows + slot_ids, -1)
        place_mat = jnp.any(row_ids[:, :, None] == jnp.arange(num_rows)[None, None, :], axis=1).astype(jnp.bfloat16)
        send_rows = jnp.einsum('tr,td->rd', place_mat, x_local, preferred_element_type=jnp.float32).astype(jnp.bfloat16)
        recv_rows = lax.all_to_all(send_rows.reshape(local_experts, ep_size, cap_rows, model_dim), 'ep', 1, 1, tiled=True)
        recv_rows = recv_rows.reshape(local_experts, ep_size * cap_rows, model_dim)
        proj_in = jnp.einsum('erd,edf->erf', recv_rows, routed_w1, preferred_element_type=jnp.float32)
        proj_gate = jnp.einsum('erd,edf->erf', recv_rows, routed_w3, preferred_element_type=jnp.float32)
        hidden = (jax.nn.silu(proj_in) * proj_gate).astype(jnp.bfloat16)
        expert_out = jnp.einsum('erf,efd->erd', hidden, routed_w2, preferred_element_type=jnp.float32).astype(jnp.bfloat16)
        back_rows = lax.all_to_all(expert_out.reshape(local_experts, ep_size, cap_rows, model_dim), 'ep', 1, 1, tiled=True)
        picked = jnp.take(back_rows.reshape(num_rows, model_dim), jnp.maximum(row_ids, 0), axis=0)
        weights = jnp.where(keep_mask, gate_vals, 0.0)
        return jnp.sum(picked.astype(jnp.float32) * weights[:, :, None], axis=1)

    def layer_local(tokens_a, tokens_b, experts_a, experts_b, gates_a, gates_b, slots_a, slots_b, shared_w1, shared_w3, shared_w2, routed_w1, routed_w3, routed_w2):
        def one_microbatch(x_local, expert_ids, gate_vals, slot_ids):
            shared_out = shared_path(x_local, shared_w1, shared_w3, shared_w2)
            routed_out = routed_path(x_local, expert_ids, gate_vals, slot_ids, routed_w1, routed_w3, routed_w2)
            return (x_local.astype(jnp.float32) + shared_out + routed_out).astype(jnp.bfloat16)
        out_a = one_microbatch(tokens_a, experts_a, gates_a, slots_a)
        out_b = one_microbatch(tokens_b, experts_b, gates_b, slots_b)
        return (out_a, out_b)

    return jax.shard_map(layer_local, mesh=mesh, in_specs=in_specs, out_specs=(tok_spec, tok_spec), check_vma=False)
```

profile of v0, /device:TPU:0, one launch (start us, length us, event | category | flops | bytes accessed | tf_op | source)
XLA Modules:
  0.0 962.2 jit_solution(10035105389887487953)
XLA Ops:
  7.2 0.7 all-gather.5.cloned.1.call-update
  8.0 0.7 all-gather.3.cloned.1.call-update
  8.7 82.8 %all-gather.5.cloned.1.call-done = bf16[2048,2048]{1,0:T(8,128)(2,1)} async-done(((bf16[32,2048]{1,0:T(8,128)(2,1)}), bf16[2048,2048]{1,0:T(8,128)(2,1)}) %all-gather.5.cloned.1.call-update) | async-done | bytes 8388624 | tf_op jit(solution)/shard_map/all_gather | solution.py:24
  91.5 6.1 fusion.30
  97.6 14.2 %fusion.4 = f32[2048,2048]{1,0:T(8,128)} fusion(bf16[88,2048]{1,0:T(8,128)(2,1)S(1)} %copy-done, bf16[2048,2048]{1,0:T(8,128)(2,1)} %all-gather.5.cloned.1.call-done, bf16[2048,88]{0,1:T(8,128)(2,1)S(1)} %copy-done.2, f32[2048,88]{0,1:T(8,128)S(1)} %fusion.30), kind=kOutput, calls=%fused_computation.14 | convolution fusion | flops 1477476352 | bytes 26607616 | tf_op jit(solution)/shard_map/dot_general | solution.py:15
  111.8 0.6 copy-done.11
  114.3 1.4 copy.56
  115.8 3.6 all-to-all-start.2
  121.5 1.5 copy.49
  123.0 4.4 all-to-all-start
  128.2 53.6 %fusion.31 = f32[30,8,1408]{2,1,0:T(8,128)S(1)} fusion(bf16[30,8,2048]{2,1,0:T(8,128)(2,1)S(1)} %reshape.42, bf16[30,2048,1408]{2,1,0:T(8,128)(2,1)} %param.27), kind=kOutput, calls=%fused_computation.67 | convolution fusion | flops 1384120320 | bytes 175349760 | tf_op jit(solution)/shard_map/erd,edf->erf/dot_general | solution.py:41
  181.9 54.7 %fusion.1 = bf16[30,8,1408]{2,1,0:T(8,128)(2,1)S(1)} fusion(bf16[30,8,2048]{2,1,0:T(8,128)(2,1)S(1)} %reshape.42, bf16[30,2048,1408]{2,1,0:T(8,128)(2,1)} %param.28, f32[30,8,1408]{2,1,0:T(8,128)S(1)} %fusion.31), kind=kOutput, calls=%fused_computation.7 | convolution fusion | flops 1386147840 | bytes 176025600 | tf_op jit(solution)/shard_map/erd,edf->erf/dot_general | solution.py:42
  236.6 6.1 fusion.28
  242.7 14.2 %fusion.5 = f32[2048,2048]{1,0:T(8,128)} fusion(bf16[88,2048]{1,0:T(8,128)(2,1)S(1)} %copy-done, bf16[2048,2048]{1,0:T(8,128)(2,1)} %all-gather.3.cloned.1.call-done, bf16[2048,88]{0,1:T(8,128)(2,1)S(1)} %copy-done.3, f32[2048,88]{0,1:T(8,128)S(1)} %fusion.28), kind=kOutput, calls=%fused_computation.15 | convolution fusion | flops 1477476352 | bytes 26607616 | tf_op jit(solution)/shard_map/dot_general | solution.py:15
  256.9 53.8 %convolution_convert_fusion.2 = bf16[30,8,2048]{2,1,0:T(8,128)(2,1)S(1)} fusion(bf16[30,8,1408]{2,1,0:T(8,128)(2,1)S(1)} %fusion.1, bf16[30,1408,2048]{2,1,0:T(8,128)(2,1)} %param.29), kind=kOutput, calls=%fused_computation.8 | convolution fusion | flops 1384611840 | bytes 174673920 | tf_op jit(solution)/shard_map/erf,efd->erd/dot_general | solution.py:44
  311.1 1.4 copy.58
  312.5 4.4 all-to-all-start.3
  316.9 1.7 copy.50
  318.9 53.6 %fusion.29 = f32[30,8,1408]{2,1,0:T(8,128)S(1)} fusion(bf16[30,8,2048]{2,1,0:T(8,128)(2,1)S(1)} %reshape.38, bf16[30,2048,1408]{2,1,0:T(8,128)(2,1)} %param.27), kind=kOutput, calls=%fused_computation.65 | convolution fusion | flops 1384120320 | bytes 175349760 | tf_op jit(solution)/shard_map/erd,edf->erf/dot_general | solution.py:41
  372.5 54.7 %fusion = bf16[30,8,1408]{2,1,0:T(8,128)(2,1)S(1)} fusion(bf16[30,8,2048]{2,1,0:T(8,128)(2,1)S(1)} %reshape.38, bf16[30,2048,1408]{2,1,0:T(8,128)(2,1)} %param.28, f32[30,8,1408]{2,1,0:T(8,128)S(1)} %fusion.29), kind=kOutput, calls=%fused_computation.6 | convolution fusion | flops 1386147840 | bytes 176025600 | tf_op jit(solution)/shard_map/erd,edf->erf/dot_general | solution.py:42
  427.1 53.6 %convolution_convert_fusion.3 = bf16[30,8,2048]{2,1,0:T(8,128)(2,1)S(1)} fusion(bf16[30,8,1408]{2,1,0:T(8,128)(2,1)S(1)} %fusion, bf16[30,1408,2048]{2,1,0:T(8,128)(2,1)} %param.29), kind=kOutput, calls=%fused_computation.9 | convolution fusion | flops 1384611840 | bytes 174673920 | tf_op jit(solution)/shard_map/erf,efd->erd/dot_general | solution.py:44
  481.2 1.4 copy.51
  482.6 3.8 all-to-all-start.1
  486.4 1.7 copy.59
  488.7 0.9 gather_fusion.1
  491.1 0.9 gather_fusion
  492.4 1.5 multiply_reduce_fusion
  493.9 1.5 multiply_reduce_fusion.1
  495.4 68.5 %reduce-scatter.5.cloned.1.call-done = f32[32,2048]{1,0:T(8,128)} async-done(((f32[2048,2048]{1,0:T(8,128)}), f32[32,2048]{1,0:T(8,128)}) %reduce-scatter.5.cloned.1.call-update) | async-done | bytes 262160 | tf_op jit(solution)/shard_map/reduce_scatter | solution.py:26
  563.9 1.6 add_convert_fusion
  565.6 388.0 %reduce-scatter.3.cloned.1.call-done = f32[32,2048]{1,0:T(8,128)} async-done(((f32[2048,2048]{1,0:T(8,128)}), f32[32,2048]{1,0:T(8,128)}) %reduce-scatter.3.cloned.1.call-update) | async-done | bytes 262160 | tf_op jit(solution)/shard_map/reduce_scatter | solution.py:26
  953.6 1.7 add_convert_fusion.1
  (84 shorter events, 8.3 us)
Async XLA Ops:
  7.2 90.4 %copy-start = (bf16[88,2048]{1,0:T(8,128)(2,1)S(1)}, bf16[88,2048]{1,0:T(8,128)(2,1)}, u32[]{:S(2)}) copy-start(bf16[88,2048]{1,0:T(8,128)(2,1)} %param.26) | copy-start | bytes 1081348
  7.2 90.4 %copy-start.2 = (bf16[2048,88]{0,1:T(8,128)(2,1)S(1)}, bf16[2048,88]{0,1:T(8,128)(2,1)}, u32[]{:S(2)}) copy-start(bf16[2048,88]{0,1:T(8,128)(2,1)} %param.25) | copy-start | bytes 1081348
  7.2 84.3 %all-gather.5.cloned.1.call-start = ((), (), s32[]{:S(2)}) async-start(), calls=%async_computation.8 | async-start | bytes 8519680 | tf_op jit(solution)/shard_map/all_gather | solution.py:24
  7.9 228.6 %all-gather.3.cloned.1.call-start = ((), (), s32[]{:S(2)}) async-start(), calls=%async_computation.6 | async-start | bytes 8519680 | tf_op jit(solution)/shard_map/all_gather | solution.py:24
  8.7 555.3 %reduce-scatter.5.cloned.1.call-start = ((), (), s32[]{:S(2)}) async-start(), calls=%async_computation.9 | async-start | bytes 17039360 | tf_op jit(solution)/shard_map/reduce_scatter | solution.py:26
  111.7 0.7 copy-start.11
  111.7 0.7 copy-start.17
  111.7 1.8 copy-start.4
  111.7 7.6 copy-start.13
  111.7 7.6 copy-start.18
  111.7 8.9 copy-start.6
  112.9 0.6 copy-start.9
  115.8 7.2 all-to-all-start.2
  120.0 0.6 copy-start.7
  123.0 189.5 %all-to-all-start = ((bf16[30,2,4,2048]{3,2,0,1:T(4,128)(2,1)}), bf16[30,2,4,2048]{3,2,0,1:T(4,128)(2,1)}, u32[]{:S(2)}, u32[]{:S(2)}) async-start(bf16[30,2,4,2048]{3,2,0,1:T(4,128)(2,1)} %copy.49), calls=%async_computation.1 | async-start | bytes 1966080 | tf_op jit(solution)/shard_map/all_to_all | solution.py:39
  127.4 826.2 %reduce-scatter.3.cloned.1.call-start = ((), (), s32[]{:S(2)}) async-start(), calls=%async_computation.7 | async-start | bytes 17039360 | tf_op jit(solution)/shard_map/reduce_scatter | solution.py:26
  236.5 6.1 copy-start.3
  312.5 170.1 %all-to-all-start.3 = ((bf16[30,2,4,2048]{3,2,0,1:T(4,128)(2,1)}), bf16[30,2,4,2048]{3,2,0,1:T(4,128)(2,1)}, u32[]{:S(2)}, u32[]{:S(2)}) async-start(bf16[30,2,4,2048]{3,2,0,1:T(4,128)(2,1)} %copy.58), calls=%async_computation.5 | async-start | bytes 1966080 | tf_op jit(solution)/shard_map/all_to_all | solution.py:45
  480.7 7.7 copy-start.10
  480.8 9.1 copy-start.20
  480.8 9.2 copy-start.12
  480.8 9.2 copy-start.15
  481.1 9.7 %copy-start.8 = (s32[32,4]{0,1:T(4,128)S(1)}, s32[32,4]{0,1:T(4,128)}, u32[]{:S(2)}) copy-start(s32[32,4]{0,1:T(4,128)} %copy-done.7) | copy-start | bytes 1540
  482.6 7.5 all-to-all-start.1
  488.2 4.0 copy-start.19
  488.2 4.1 copy-start.14
  488.2 4.1 copy-start.16
  488.6 466.6 %copy-start.1 = (bf16[88,2048]{1,0:T(8,128)(2,1)S(1)}, bf16[88,2048]{1,0:T(8,128)(2,1)}, u32[]{:S(2)}) copy-start(bf16[88,2048]{1,0:T(8,128)(2,1)} %param.26) | copy-start | bytes 1081348
  488.7 75.3 %copy-start.5 = (bf16[32,2048]{1,0:T(8,128)(2,1)S(1)}, bf16[32,2048]{1,0:T(8,128)(2,1)}, u32[]{:S(2)}) copy-start(bf16[32,2048]{1,0:T(8,128)(2,1)} %param.17) | copy-start | bytes 393220
Sparse Core Ops, SparseCore 0:
  10.9 80.5 all-gather.4
  94.3 77.6 all-gather.2
  174.4 389.4 reduce-scatter.4
  566.2 387.3 reduce-scatter.2
where the time goes:
time: 968 us; the launch traced here: 962 us
  waiting for transfers between devices  541 us (56%)
  matrix products  365 us (38%)
  local copies, waits for them, and re-layouts  17.4 us (2%)
  starting transfers between devices  16.5 us (2%)
  between operations  14.7 us (2%)
    reduce_scatter x2, waiting for transfers between devices, shared_path(): return lax.psum_scatter(partial_sum, 'tp', scatter_dimension=0, tiled=True)  457 us
    dot_general x2, matrix products, routed_path(): jnp.einsum('erd,edf->erf', recv_rows, routed_w3, preferred_element_type=j...  109 us
    dot_general x2, matrix products, routed_path(): jnp.einsum('erf,efd->erd', hidden, routed_w2, preferred_element_type=jnp....  107 us
    dot_general x2, matrix products, routed_path(): jnp.einsum('erd,edf->erf', recv_rows, routed_w1, preferred_element_type=j...  107 us
    all_gather x2, waiting for transfers between devices, shared_path(): gathered = lax.all_gather(x_local, 'tp', axis=0, tiled=True)  82.8 us
    dot_general x2, matrix products, swiglu_rows(): return jnp.dot(hidden, w_out, preferred_element_type=jnp.float32)  28.3 us
  transfers between devices with their start and end apart: 8, of which 3 were waited for; matrix products, arithmetic and copies ran while one was open for 40% of the time, Pallas kernels for 0%

commit v1 on v0

v1 whole, which is shorter than its diff:
```python
import functools

import jax
import jax.numpy as jnp
from jax import lax
from jax.experimental import pallas as pl
from jax.experimental.pallas import tpu as pltpu
from jax.sharding import PartitionSpec as P

MESH = pl.DeviceIdType.MESH
BF16 = jnp.bfloat16
F32 = jnp.float32
LANES = 128
CHUNK = 256
STRIDE = (1, 4, 16)
SIDE = 4
CUBE = 8
HALF = 48


def capacity_rows(tok_local, top_k, num_experts):
    return max(4, (2 * tok_local * top_k) // num_experts)


def column_parts(width, order):
    tiles = width // LANES
    size = [tiles // 3] * 3
    for i in range(tiles % 3):
        size[order[i]] += 1
    starts = [0, size[0], size[0] + size[1]]
    return [(s * LANES, n * LANES) for s, n in zip(starts, size) if True]


def weight_of(t):
    return 4 - 2 * t + (t * (t - 1)) // 2


def kernel(cfg, ta, tb, ma, mb, w1, w3, w2, rw1, rw3, rw2, oa, ob,
           xg, wg13, wg2, h, hs, gm, rd, r1, r2, r3,
           loc_sem, wl_sem, w2_sem, ag_s, ag_r, g13_s, g13_r, g2_s, g2_r, xd_s, xd_r, rd_s, rd_r, rs_s, rs_r):
    tok, dim, ff, sff, n_local, cap, width = (cfg[k] for k in ("tok", "dim", "ff", "sff", "n_local", "cap", "width"))
    experts_here = cfg["experts_here"]
    n_chunks = dim // CHUNK
    per_chunk = CHUNK // LANES
    xcols = column_parts(dim + LANES, (0, 2, 1))
    wcols = column_parts(dim, (1, 0, 2))

    tp = lax.axis_index("tp")
    core = lax.axis_index("ep")
    coord = [tp % SIDE, (tp // SIDE) % SIDE, tp // (SIDE * SIDE)]
    near = [[tp + (1 - 2 * (c % 2)) * s for c, s in zip(coord, STRIDE)],
            [tp + (3 - 2 * c) * s for c, s in zip(coord, STRIDE)]]
    place = coord[0] % 2 + 2 * (coord[1] % 2) + 4 * (coord[2] % 2)

    def at(chip):
        return {"tp": chip, "ep": core}

    partner = {"tp": tp, "ep": 1 - core}

    def token_chip(m, d):
        n0, n1, n2 = near[m]
        return n0 + d * (n1 - n0) + ((d * (d - 1)) // 2) * (n2 - 2 * n1 + n0)

    def remote(src, dst, s, r, where):
        return pltpu.make_async_remote_copy(src_ref=src, dst_ref=dst, send_sem=s, recv_sem=r, device_id=where, device_id_type=MESH)

    def items_of(p, s):
        got = [0]
        for t in range(s):
            got = got + [i | (1 << ((p + t) % 3)) for i in got]
        return got

    def x_copy(m, p, s, i):
        d = (p + s) % 3
        to = i | (1 << d)
        c0, n = xcols[p]
        return remote(xg.at[m, pl.ds(i * tok, tok), pl.ds(c0, n)], xg.at[m, pl.ds(to * tok, tok), pl.ds(c0, n)],
                      ag_s.at[m, p, to], ag_r.at[m, p, to], at(near[m][d]))

    def w13_copy(m, p, s, i):
        d = (p + s) % 3
        to = i | (1 << d)
        c0, n = wcols[p]
        return remote(wg13.at[m, :, pl.ds(i * HALF, HALF), pl.ds(c0, n)], wg13.at[m, :, pl.ds(to * HALF, HALF), pl.ds(c0, n)],
                      g13_s.at[m, p, to], g13_r.at[m, p, to], at(near[1 - m][d]))

    def w2_copy(m, p, s, i):
        d = (p + s) % 3
        to = i | (1 << d)
        c0, n = wcols[p]
        return remote(wg2.at[m, pl.ds(i * HALF, HALF), pl.ds(c0, n)], wg2.at[m, pl.ds(to * HALF, HALF), pl.ds(c0, n)],
                      g2_s.at[m, p, to], g2_r.at[m, p, to], at(near[1 - m][d]))

    def step(copy, s, what):
        for m in range(2):
            for p in range(3):
                for i in items_of(p, s):
                    c = copy(m, p, s, i)
                    if what == "start":
                        c.start()
                    elif what == "recv":
                        c.wait_recv()
                    else:
                        c.wait_send()

    half_rows = CUBE * tok

    def x_swap(m):
        return remote(xg.at[m, pl.ds(0, half_rows)], xg.at[m, pl.ds(half_rows, half_rows)], xd_s.at[m], xd_r.at[m], partner)

    barrier = pltpu.get_barrier_semaphore()
    for kind in range(2):
        for d in range(3):
            pl.semaphore_signal(barrier, inc=1, device_id=at(near[kind][d]), device_id_type=MESH)
    pl.semaphore_signal(barrier, inc=1, device_id=partner, device_id_type=MESH)

    own = []
    for m, (t, meta) in enumerate(((ta, ma), (tb, mb))):
        own.append(pltpu.make_async_copy(t, xg.at[m, pl.ds(0, tok), pl.ds(0, dim)], loc_sem.at[2 * m]))
        own.append(pltpu.make_async_copy(meta, xg.at[m, pl.ds(0, tok), pl.ds(dim, LANES)], loc_sem.at[2 * m + 1]))

    def expert_row(j):
        return (place + CUBE * j) % n_local

    def first_stage(slots, xe, wt1, wt3, wt2):
        shared_in = [pltpu.make_async_copy(src, dst, loc_sem.at[4 + k]) for k, (src, dst) in enumerate(((w1, wt1), (w3, wt3), (w2, wt2)))]

        def routed_in(j):
            e = expert_row(j)
            slot = j % 2
            return [pltpu.make_async_copy(src.at[e], slots.at[slot, k], wl_sem.at[slot, k]) for k, src in enumerate((rw1, rw3))]

        for c in own + shared_in:
            c.start()
        for j in range(2):
            for c in routed_in(j):
                c.start()

        row = lax.broadcasted_iota(jnp.int32, (HALF, sff), 0)
        col = lax.broadcasted_iota(jnp.int32, (HALF, sff), 1)
        pick = (col == row + HALF * core).astype(BF16)
        for c in own:
            c.wait()
        for k, src in enumerate((wt1, wt3)):
            shared_in[k].wait()
            mine = lax.dot_general(pick, src[...], (((1,), (1,)), ((), ())), preferred_element_type=F32).astype(BF16)
            for m in range(2):
                wg13[m, k, 0:HALF, :] = mine
        shared_in[2].wait()
        mine = jnp.dot(pick, wt2[...], preferred_element_type=F32).astype(BF16)
        for m in range(2):
            wg2[m, 0:HALF, :] = mine

        pl.semaphore_wait(barrier, 7)

        step(x_copy, 0, "start")
        step(w13_copy, 0, "start")
        step(w2_copy, 0, "start")
        step(x_copy, 0, "recv")
        step(x_copy, 1, "start")
        step(w13_copy, 0, "recv")
        step(w13_copy, 1, "start")
        step(x_copy, 1, "recv")
        step(x_copy, 2, "start")
        step(w2_copy, 0, "recv")
        step(w2_copy, 1, "start")
        step(w13_copy, 1, "recv")
        step(w13_copy, 2, "start")
        step(x_copy, 2, "recv")
        for m in range(2):
            x_swap(m).start()
        for m in range(2):
            x_swap(m).wait_recv()
        step(w2_copy, 1, "recv")
        step(w2_copy, 2, "start")

        block = 4 * tok
        lane = lax.broadcasted_iota(jnp.int32, (block, 2 * LANES), 1)
        token = lax.broadcasted_iota(jnp.int32, (block, 2 * LANES), 0)
        per = 4 * cap
        span = experts_here * per
        part = lane // span
        in_part = lane % span
        near_expert = place + CUBE * (in_part // per)
        expert = core * n_local + near_expert + jnp.where(near_expert >= n_local, 1000, 0)
        key_of = jnp.where((in_part % per) // cap == token // tok, expert * cap + in_part % cap, -5).astype(F32)
        for m in range(2):
            for b in range(4):
                meta = xg[m, b * block:(b + 1) * block, dim:dim + LANES].astype(F32)
                hit = jnp.zeros((block, 2 * LANES), F32)
                gate = jnp.zeros((block, 2 * LANES), F32)
                for k in range(4):
                    same = meta[:, k:k + 1] == key_of
                    g = jnp.where(part == 0, meta[:, 4 + k:5 + k],
                                  jnp.where(part == 1, meta[:, 8 + k:9 + k], jnp.where(part == 2, meta[:, 12 + k:13 + k], 0.0)))
                    hit = jnp.where(same, 1.0, hit)
                    gate = jnp.where(same, g, gate)
                gm[m * 4 + b] = gate.astype(BF16)
                put = hit[:, :span].astype(BF16)
                rows = lax.dot_general(put, xg[m, b * block:(b + 1) * block, 0:dim], (((0,), (0,)), ((), ())),
                                       preferred_element_type=F32).astype(BF16)
                for j in range(experts_here):
                    r0 = (m * 4 + b) * per
                    xe[j, r0:r0 + per, :] = rows[j * per:(j + 1) * per]

        @pl.loop(0, experts_here)
        def _(j):
            slot = j % 2
            for c in routed_in(j):
                c.wait()
            for o in range(0, ff, CHUNK):
                n = min(CHUNK, ff - o)
                a = jnp.dot(xe[j], slots[slot, 0, :, o:o + n], preferred_element_type=F32)
                g = jnp.dot(xe[j], slots[slot, 1, :, o:o + n], preferred_element_type=F32)
                h[j, :, o:o + n] = (jax.nn.silu(a) * g).astype(BF16)

            @pl.when(j + 2 < experts_here)
            def _():
                for c in routed_in(j + 2):
                    c.start()

    pl.run_scoped(
        first_stage,
        pltpu.VMEM((2, 2, dim, ff), BF16),
        pltpu.VMEM((experts_here, 8 * 4 * cap, dim), BF16),
        pltpu.VMEM((dim, sff), BF16),
        pltpu.VMEM((dim, sff), BF16),
        pltpu.VMEM((sff, dim), BF16),
    )

    def second_stage(w2b, acc, sd, rr):
        def w2_in(n):
            cols = pl.ds(pl.multiple_of(n * CHUNK, CHUNK), CHUNK)
            return [pltpu.make_async_copy(rw2.at[expert_row(j), :, cols], w2b.at[n, j], w2_sem.at[n, j]) for j in range(experts_here)]

        @pl.loop(0, n_chunks)
        def _(n):
            for c in w2_in(n):
                c.start()

        rr[...] = jnp.zeros_like(rr)

        step(w13_copy, 2, "recv")
        rows = 2 * CUBE * tok // 2
        for m in range(2):
            @pl.loop(0, 2)
            def _(b):
                mine = pl.ds(pl.multiple_of(b * rows, rows), rows)
                x = xg[m, mine, 0:dim]
                a = lax.dot_general(x, wg13[m, 0], (((1,), (1,)), ((), ())), preferred_element_type=F32)
                g = lax.dot_general(x, wg13[m, 1], (((1,), (1,)), ((), ())), preferred_element_type=F32)
                hs[m, mine, :] = (jax.nn.silu(a) * g).astype(BF16)

        step(w2_copy, 2, "recv")

        block = 4 * tok
        per = 4 * cap
        span = experts_here * per
        full = CUBE * tok

        def d2d(n):
            return remote(sd.at[n], rd.at[n], rd_s.at[n], rd_r.at[n], partner)

        def halving(s, n, m, u):
            q = n * per_chunk + u
            rows = full >> (s + 1)
            dst = (r1, r2, r3)[s]
            return remote(acc.at[q, m, pl.ds(rows, rows)], dst.at[q, m], rs_s.at[s, q, m], rs_r.at[s, q, m], at(token_chip(m, (q + s) % 3)))

        def compute(n):
            for c in w2_in(n):
                c.wait()
            cols = pl.ds(pl.multiple_of(n * CHUNK, CHUNK), CHUNK)
            for j in range(experts_here):
                out = jnp.dot(h[j], w2b[n, j], preferred_element_type=F32).astype(BF16)
                for k in range(8):
                    for part in range(3):
                        r0 = part * span + j * per
                        rr[k, r0:r0 + per, :] = out[k * per:(k + 1) * per]
            lead = []
            for u in range(per_chunk):
                rho = (n * per_chunk + u) % 3
                lead.append([weight_of((i - rho + 3) % 3) for i in range(3)])
            for m in range(2):
                for b in range(4):
                    o = jnp.dot(hs[m, b * block:(b + 1) * block, :], wg2[m, :, cols], preferred_element_type=F32)
                    o += jnp.dot(gm[m * 4 + b], rr[m * 4 + b], preferred_element_type=F32)
                    for i in range(4):
                        r = (b % 2) * 4 + i
                        for u in range(per_chunk):
                            pos = sum(lead[u][bit] for bit in range(3) if r >> bit & 1)
                            where = pl.ds(pl.multiple_of(pos * tok, tok), tok) if r else pl.ds(0, tok)
                            piece = o[i * tok:(i + 1) * tok, u * LANES:(u + 1) * LANES]
                            if b < 2:
                                acc[n * per_chunk + u, m, where, :] = piece
                            else:
                                sd[n, m, u, where, :] = piece
            d2d(n).start()

        def each(n, f):
            for u in range(per_chunk):
                for m in range(2):
                    f(n * per_chunk + u, m, u)

        def from_partner(n):
            d2d(n).wait_recv()

            def f(q, m, u):
                acc[q, m] += rd[n, m, u]
                halving(0, n, m, u).start()
            each(n, f)

        def from_neighbour(s, n):
            def f(q, m, u):
                halving(s, n, m, u).wait_recv()
                rows = full >> (s + 1)
                acc[q, m, 0:rows, :] += (r1, r2)[s][q, m]
                halving(s + 1, n, m, u).start()
            each(n, f)

        def finish(n):
            def f(q, m, u):
                halving(2, n, m, u).wait_recv()
                cols = pl.ds(pl.multiple_of(q * LANES, LANES), LANES)
                y = acc[q, m, 0:tok, :] + r3[q, m] + xg[m, 0:tok, cols].astype(F32)
                (oa, ob)[m][:, cols] = y.astype(BF16)
            each(n, f)

        stages = [(0, compute), (1, from_partner), (3, functools.partial(from_neighbour, 0)), (5, functools.partial(from_neighbour, 1)), (7, finish)]

        @pl.loop(0, n_chunks + 7)
        def _(t):
            for lag, f in stages:
                @pl.when((t >= lag) & (t < n_chunks + lag))
                def _(lag=lag, f=f):
                    f(t - lag)

        @pl.loop(0, n_chunks)
        def _(n):
            d2d(n).wait_send()
            for s in range(3):
                each(n, lambda q, m, u: halving(s, n, m, u).wait_send())

    pl.run_scoped(
        second_stage,
        pltpu.VMEM((n_chunks, experts_here, ff, CHUNK), BF16),
        pltpu.VMEM((n_chunks * per_chunk, 2, CUBE * tok, LANES), F32),
        pltpu.VMEM((n_chunks, 2, per_chunk, CUBE * tok, LANES), F32),
        pltpu.VMEM((8, 2 * LANES, CHUNK), BF16),
    )

    for s in range(3):
        step(x_copy, s, "send")
        step(w13_copy, s, "send")
        step(w2_copy, s, "send")
    for m in range(2):
        x_swap(m).wait_send()


def routing_meta(expert_ids, gate_vals, slot_ids, cap):
    key = jnp.where(slot_ids >= 0, expert_ids * cap + slot_ids, -1).astype(F32)
    top = jnp.minimum(lax.reduce_precision(gate_vals, 8, 7), float(jnp.finfo(BF16).max))
    mid = lax.reduce_precision(gate_vals - top, 8, 7)
    low = lax.reduce_precision(gate_vals - top - mid, 8, 7)
    meta = jnp.concatenate([key, top, mid, low], axis=1)
    return jnp.pad(meta, ((0, 0), (0, LANES - meta.shape[1]))).astype(BF16)


def solution(mesh):
    ep_size = mesh.shape['ep']
    tok_spec = P(('data', 'ep', 'tp'), None)
    in_specs = (tok_spec,) * 8 + (P(None, 'tp'), P(None, 'tp'), P('tp', None), P('ep', None, None), P('ep', None, None), P('ep', None, None))

    def layer_local(tokens_a, tokens_b, experts_a, experts_b, gates_a, gates_b, slots_a, slots_b, shared_w1, shared_w3, shared_w2, routed_w1, routed_w3, routed_w2):
        tok, dim = tokens_a.shape
        n_local, _, ff = routed_w1.shape
        sff = shared_w1.shape[1]
        cap = capacity_rows(tok, experts_a.shape[1], n_local * ep_size)
        experts_here = -(-n_local // CUBE)
        cfg = dict(tok=tok, dim=dim, ff=ff, sff=sff, n_local=n_local, cap=cap, experts_here=experts_here, width=CUBE * HALF)
        meta_a = routing_meta(experts_a, gates_a, slots_a, cap)
        meta_b = routing_meta(experts_b, gates_b, slots_b, cap)
        n_chunks = dim // CHUNK
        n_q = dim // LANES
        dma = pltpu.SemaphoreType.DMA
        any_spec = pl.BlockSpec(memory_space=pl.ANY)
        return pl.pallas_call(
            functools.partial(kernel, cfg),
            out_shape=[jax.ShapeDtypeStruct((tok, dim), BF16)] * 2,
            in_specs=[any_spec] * 10,
            out_specs=[pl.BlockSpec(memory_space=pltpu.VMEM)] * 2,
            scratch_shapes=[
                pltpu.VMEM((2, 2 * CUBE * tok, dim + LANES), BF16),
                pltpu.VMEM((2, 2, CUBE * HALF, dim), BF16),
                pltpu.VMEM((2, CUBE * HALF, dim), BF16),
                pltpu.VMEM((experts_here, 8 * 4 * cap, ff), BF16),
                pltpu.VMEM((2, 2 * CUBE * tok, CUBE * HALF), BF16),
                pltpu.VMEM((8, 4 * tok, 2 * LANES), BF16),
                pltpu.VMEM((n_chunks, 2, CHUNK // LANES, CUBE * tok, LANES), F32),
                pltpu.VMEM((n_q, 2, CUBE * tok // 2, LANES), F32),
                pltpu.VMEM((n_q, 2, CUBE * tok // 4, LANES), F32),
                pltpu.VMEM((n_q, 2, CUBE * tok // 8, LANES), F32),
                dma((8,)),
                dma((2, 2)),
                dma((n_chunks, experts_here)),
                dma((2, 3, CUBE)), dma((2, 3, CUBE)),
                dma((2, 3, CUBE)), dma((2, 3, CUBE)),
                dma((2, 3, CUBE)), dma((2, 3, CUBE)),
                dma((2,)), dma((2,)),
                dma((n_chunks,)), dma((n_chunks,)),
                dma((3, n_q, 2)), dma((3, n_q, 2)),
            ],
            compiler_params=pltpu.CompilerParams(collective_id=0, has_side_effects=True, vmem_limit_bytes=67043328),
            name="expert_layer",
        )(tokens_a, tokens_b, meta_a, meta_b, shared_w1, shared_w3, shared_w2, routed_w1, routed_w3, routed_w2)

    return jax.shard_map(layer_local, mesh=mesh, in_specs=in_specs, out_specs=(tok_spec, tok_spec), check_vma=False)
```

time: 968 us -> 102 us (0.11)
  waiting for transfers between devices: 541 us -> 0 us
  matrix products: 365 us -> 0 us
  Pallas kernels: 0 us -> 84.8 us
  starting transfers between devices: 16.5 us -> 0 us
  between operations: 14.7 us -> 0.65 us
    reduce_scatter x2 -> x0, waiting for transfers between devices: 457 us -> none  [shared_path(): return lax.psum_scatter(partial_sum, 'tp', scatter_dimension=0, tiled=True)]
    dot_general x12 -> x0, matrix products: 365 us -> none  [the longest x2 109 us: routed_path(): jnp.einsum('erd,edf->erf', recv_rows, routed_w3, preferred_element_type=j...]
    pallas_call x0 -> x1, Pallas kernels: none -> 84.8 us  [layer_local(): pl.pallas_call(functools.partial(kernel, cfg), out_shape=[jax.ShapeDtypeS...]
    all_gather x2 -> x0, waiting for transfers between devices: 82.8 us -> none  [shared_path(): gathered = lax.all_gather(x_local, 'tp', axis=0, tiled=True)]
    all_to_all x4 -> x0, starting transfers between devices: 16.2 us -> none  [the longest x2 8.21 us: routed_path(): lax.all_to_all(expert_out.reshape(local_experts, ep_size, cap_rows, model...]
  transfers between devices with their start and end apart: 8 -> 0, of which waited for: 3 -> 0; matrix products, arithmetic and copies ran while one was open for 40% -> 0% of each run, Pallas kernels for 0% -> 0%
where the time goes in v1:
time: 102 us; the launch traced here: 101 us
  Pallas kernels  84.8 us (83%)
  local copies, waits for them, and re-layouts  10.7 us (10%)
  other arithmetic  4.85 us (5%)
    pallas_call x1, Pallas kernels, layer_local(): pl.pallas_call(functools.partial(kernel, cfg), out_shape=[jax.ShapeDtypeS...  84.8 us
    unnamed x8, local copies, waits for them, and re-layouts  10.1 us

profile of v1, /device:TPU:0, one launch (start us, length us, event | category | flops | bytes accessed | tf_op | source)
XLA Modules:
  0.0 101.0 jit_solution(14928559957536349176)
XLA Ops:
  0.6 0.7 broadcast_compare_fusion.1
  1.3 0.7 broadcast_compare_fusion
  2.0 0.7 broadcast_multiply_fusion.1
  2.7 0.7 broadcast_multiply_fusion
  3.4 0.7 reduce_precision.18
  4.1 0.7 reduce_precision.21
  4.7 0.1 copy.39
  4.8 0.1 copy.34
  4.9 0.1 copy.40
  5.0 0.1 copy.35
  5.1 0.1 copy.37
  5.2 0.1 copy.32
  5.3 0.8 copy.36
  6.1 0.8 copy.41
  6.9 0.8 copy.33
  7.6 0.8 copy.38
  8.4 0.7 fusion.14
  9.1 2.0 %copy.42.w1 = bf16[2048,88]{1,0:T(8,128)(2,1)} copy(bf16[2048,88]{0,1:T(8,128)(2,1)} %param.22) | data formatting | bytes 720896 | tf_op args[8]
  11.1 2.0 %copy.43.w3 = bf16[2048,88]{1,0:T(8,128)(2,1)} copy(bf16[2048,88]{0,1:T(8,128)(2,1)} %param.23) | data formatting | bytes 720896 | tf_op args[9]
  13.1 84.8 %expert_layer.1 = (bf16[32,2048]{1,0:T(8,128)(2,1)}, bf16[32,2048]{1,0:T(8,128)(2,1)}) custom-call(bf16[32,2048]{1,0:T(8,128)(2,1)} %ta.1, bf16[32,2048]{1,0:T(8,128)(2,1)} %tb.1, bf16[32,128]{1,0:T(8,128)(2,1)} %get-tuple-element.6.ma, bf16[32,128]{1,0:T(8,128)(2,1)} %get-tuple-element.7.mb, bf16[2048,88]{1,0:T(8,128)(2,1)} %copy.42.w1, ...), custom_call_target="tpu_custom_call" | custom-call | tf_op jit(solution)/shard_map/expert_layer/pallas_call | solution.py:387
  97.9 1.6 %copy.46 = bf16[32,2048]{1,0:T(8,128)(2,1)} copy(bf16[32,2048]{1,0:T(8,128)(2,1)} %get-tuple-element.10) | data formatting | bytes 262144
  99.5 1.6 %copy.47 = bf16[32,2048]{1,0:T(8,128)(2,1)} copy(bf16[32,2048]{1,0:T(8,128)(2,1)} %get-tuple-element.11) | data formatting | bytes 262144
  (6 shorter events, 0.1 us)
